TPU v7x, 32 devices: a whole 2x2x4 slice. The times are simulated.
32 devices in a mesh: gx: 4 (over y, core), gy: 4 (over z), gz: 2 (over x).
Axes of the slice: x: 2, y: 2, z: 4, core: 2. Of those that a mesh axis runs over, the one named last changes fastest.
Arguments:
- spin_vectors: float32 [2, 3, 32, 32, 256], P(None, None, 'gx', 'gy', 'gz'), may hold values from -1 to 1, as said below
- displacement: float32 [2, 3, 32, 32, 256], P(None, None, 'gx', 'gy', 'gz'), may hold values from -0.15 to 0.15
- occupied: int32 [2, 32, 32, 256], P(None, 'gx', 'gy', 'gz'), may hold values 0 or 1
- applied_field: float32 [3], replicated, may hold values from -4 to 4
Outputs:
- new_spins: float32 [2, 3, 32, 32, 256], P(None, None, 'gx', 'gy', 'gz')
- forces: float32 [2, 3, 32, 32, 256], P(None, None, 'gx', 'gy', 'gz')
Inputs may be any that keep to these rules, and one draw needn't show every extreme that they name: `occupied`: 1 where a lattice site holds an atom, 0 at a vacancy. `spin_vectors`: every spin vector has unit length.
All inputs are finite; a program needn't handle non-finite values. No bound on the sum of `occupied` on one device may be relied on, other than what follows from the above.
Results may differ from a plain program's by a relative error of at most 0.0001.
Values sent between devices are 32-bit elements; how exact they have to be, the bound alone decides.
A program may use at most 64 MiB of HBM per device.

v0:
```python
import functools
import itertools

import jax
import jax.numpy as jnp
from jax import lax
from jax.experimental import pallas as pl
from jax.experimental.pallas import tpu as pltpu
from jax.sharding import PartitionSpec as P

step_time = 0.6
exchange_scale = 0.35
exchange_decay = 4.0
pair_scale = 0.5
pair_decay = 6.0
density_decay = 3.0
bond_length = 0.8660254037844386
corner_offsets = list(itertools.product((0, 1), repeat=3))
axes = ("gx", "gy", "gz")
MESH = pl.DeviceIdType.MESH

DISPLACED, SPUN = 0, 1
GROUPS = ((0, 4), (9, 3))
ARRAYS = 16


def fields_of(group):
    first, n = GROUPS[group]
    return [(first + n * s + f, 7 * s + f + (3 if group == DISPLACED else 0), s) for s in range(2) for f in range(n)]


def strip_of(group):
    first, n = GROUPS[group]
    return first + 2 * n


TO_BELOW = tuple(
    [(i // 4, i, 0, 2, 2 * (i % 4)) for i in range(8)] + [(2, 2 + i, 2, 2, 2 * i) for i in range(4)])
TO_ABOVE_0 = tuple([(0, i, 7, 1, i) for i in range(8)] + [(1, 2 + i, 5, 2, 2 * i) for i in range(4)])
TO_ABOVE_1 = tuple(
    [(i // 4, i, 6, 2, 2 * (i % 4)) for i in range(8)] + [(2, 2 + i, 4, 2, 2 * i) for i in range(4)])


@functools.cache
def turned_planes():
    need = {(0, x, y) for x in range(9) for y in range(9)} | {(1, x, y) for x in range(-1, 8) for y in range(-1, 8)}
    need |= {(b, x, y) for b in (0, 1) for x in range(8) for y in range(8)}
    planes = {}
    for u in reversed(range(15)):
        sector = u if u < 8 else 14 - u
        sub, quarter = sector % 2, sector // 2
        turned = [k for k in need if k[0] == sub and k[1] // 4 % 2 + 2 * (k[2] // 4 % 2) == quarter]
        planes[u] = sorted({k[1] for k in turned})
        for _, x, y in turned:
            for a, b, _ in corner_offsets:
                need.add((1, x - a, y - b) if sub == 0 else (0, x + a, y + b))
    return planes


def working(rows, lanes):
    row = lax.broadcasted_iota(jnp.int32, (rows, lanes), 0)
    first, last = row % 4 == 0, row % 4 == 3

    def turn(v, n):
        return pltpu.roll(v, n % rows, 0)

    def below(pair, tile):
        a, b = pair
        if tile == 0:
            return jnp.where(first, turn(b, 5), turn(a, 1))
        return jnp.where(first, turn(a, 1), turn(b, 1))

    def above(pair, tile):
        a, b = pair
        if tile == 0:
            return jnp.where(last, turn(b, -1), turn(a, -1))
        return jnp.where(last, turn(a, 3), turn(b, -1))

    def z_below(v):
        return pltpu.roll(v, 1, 1)

    def z_above(v):
        return pltpu.roll(v, lanes - 1, 1)

    return below, above, z_below, z_above


def place_rows():
    up, down, at, n_up, n_down = [], [], [], 0, 0
    for group in (DISPLACED, SPUN):
        for s in [s for _, _, s in fields_of(group)] + [1]:
            up.append(n_up)
            down.append(n_down)
            at.append(s)
            n_up += 2 + s
            n_down += 3
    return up + [n_up], down + [n_down], at


UP, DOWN, GEOMETRY = place_rows()


def kernel(sizes, spin_in, disp_in, occ_in, field, out_s, out_f, E, PZ, RZ, SU, RU, SD, RD, SX, RX, SC, RC, W, WZ, J, J1, P3, RI, FS, FZ, ACC,
           spin, disp, occ, send_sem, recv_sem, load_sem):
    nx, ny, nz = sizes
    me = {a: lax.axis_index(a) for a in axes}
    count = dict(zip(axes, sizes))

    def peer(axis, step):
        n = count[axis]
        return {axis: lax.rem(me[axis] + (n + step), n)}

    peers = []
    for axis in axes:
        peers.append(peer(axis, 1))
        if count[axis] > 2:
            peers.append(peer(axis, -1))
    barrier = pltpu.get_barrier_semaphore()
    for p in peers:
        pl.semaphore_signal(barrier, inc=1, device_id=p, device_id_type=MESH)

    loads = [pltpu.make_async_copy(a, b, load_sem.at[i])
             for i, (a, b) in enumerate(((spin_in, spin), (disp_in, disp), (occ_in, occ)))]
    for c in loads:
        c.start()
    for c in loads:
        c.wait()

    lane = lax.broadcasted_iota(jnp.int32, (8, 128), 1)
    row = lax.broadcasted_iota(jnp.int32, (8, 128), 0)
    upper = row < 4

    def swap(v):
        return pltpu.roll(v, 4, 0)

    def load_own(x, _):
        for group in (DISPLACED, SPUN):
            packed = jnp.zeros((8, 128), jnp.float32)
            for n, (e, w, s) in enumerate(fields_of(group)):
                f = w % 7
                if f < 3:
                    v = spin[s, f, x]
                elif f < 6:
                    v = disp[s, f - 3, x]
                else:
                    v = occ[s, x].astype(jnp.float32)
                E[e, x, 0] = v
                packed = jnp.where(lane // 16 == n, pltpu.roll(v, (8 + 16 * n) % 128, 1), packed)
            PZ[group, x] = packed
        return 0

    lax.fori_loop(0, 8, load_own, 0, unroll=2)
    inner = (row >= 2) & (row < 6)

    def routes(e):
        return ((SU, RU, UP[e], (TO_ABOVE_0, TO_ABOVE_1)[GEOMETRY[e]]), (SD, RD, DOWN[e], TO_BELOW))

    def pack_rows(e):
        own = [E[e, x, 0] for x in range(8)]
        for out, _unused, first, pieces in routes(e):
            tiles = {}
            for tile, x, low, n, to in pieces:
                v = pltpu.roll(own[x], (to - low) % 8, 0)
                tiles[tile] = jnp.where(row < to, tiles[tile], v) if to else v
            for tile, v in tiles.items():
                out[first + tile] = v
        SX[0, e] = jnp.where(inner, own[2], swap(own[3]))
        SX[1, e] = jnp.where(inner, own[4], swap(own[5]))

    def unpack_rows(e):
        rows = [jnp.zeros((8, 128), jnp.float32)] * 8
        for _unused, arrived, first, pieces in routes(e):
            for tile, x, low, n, to in pieces:
                v = pltpu.roll(arrived[first + tile], (low - to) % 8, 0)
                rows[x] = jnp.where((row >= low) & (row < low + n), v, rows[x])
        for x in range(8):
            E[e, x, 1] = rows[x]
        SC[0, e] = jnp.where(inner, swap(rows[1]), rows[0])
        SC[1, e] = jnp.where(inner, swap(rows[7]), rows[6])

    def arrays_of(group):
        return range(GROUPS[group][0], strip_of(group) + 1)

    for group in (DISPLACED, SPUN):
        for e, _, _ in fields_of(group):
            pack_rows(e)
    pl.semaphore_wait(barrier, len(peers))

    def send(i, src, dst, to):
        c = pltpu.make_async_remote_copy(
            src_ref=src, dst_ref=dst, send_sem=send_sem.at[i], recv_sem=recv_sem.at[i],
            device_id=to, device_id_type=MESH)
        c.start()
        return c

    def exchange_y(i, lo, hi):
        up = pl.ds(UP[lo], UP[hi] - UP[lo])
        down = pl.ds(DOWN[lo], DOWN[hi] - DOWN[lo])
        return [
            send(i, SD.at[down], RD.at[down], peer("gy", -1)),
            send(i + 1, SU.at[up], RU.at[up], peer("gy", 1)),
        ]

    def exchange_x(i, lo, hi):
        part = pl.ds(lo, hi - lo)

        def plane(x):
            return E.at[part, pl.ds(x, 2), 0]

        return [
            send(i, plane(0), plane(8), peer("gx", -1)),
            send(i + 1, plane(6), plane(14), peer("gx", 1)),
            send(i + 2, SX.at[0, part], RX.at[0, part], peer("gx", -1)),
            send(i + 3, SX.at[1, part], RX.at[1, part], peer("gx", 1)),
        ]

    def exchange_z(i, group):
        found = [send(i, PZ.at[group], RZ.at[0, group], peer("gz", -1))]
        if nz > 2:
            found.append(send(i + 1, PZ.at[group], RZ.at[1, group], peer("gz", 1)))
        return found

    def take_strips(group, copies):
        for c in copies:
            c.wait()
        for x in range(8):
            v = RZ[0, group, x]
            if nz > 2:
                v = jnp.where(lane % 16 < 8, RZ[1, group, x], v)
            E[strip_of(group), x, 0] = v
        pack_rows(strip_of(group))

    def corner_copies(i, group):
        part = pl.ds(GROUPS[group][0], len(arrays_of(group)))
        return [send(i + n, SC.at[n, part], RC.at[n, part], peer("gx", 2 * n - 1)) for n in range(2)]

    z0 = exchange_z(0, DISPLACED)
    ys0 = exchange_y(4, GROUPS[0][0], strip_of(0))
    xs0 = exchange_x(12, GROUPS[0][0], strip_of(0))
    z1 = exchange_z(2, SPUN)
    take_strips(DISPLACED, z0)
    ys0 += exchange_y(6, strip_of(0), strip_of(0) + 1)
    ys1 = exchange_y(8, GROUPS[1][0], strip_of(1))
    xs0 += exchange_x(16, strip_of(0), strip_of(0) + 1)
    xs1 = exchange_x(20, GROUPS[1][0], strip_of(1))
    take_strips(SPUN, z1)
    ys1 += exchange_y(10, strip_of(1), strip_of(1) + 1)
    xs1 += exchange_x(24, strip_of(1), strip_of(1) + 1)
    for c in ys0:
        c.wait()
    for e in arrays_of(DISPLACED):
        unpack_rows(e)
    corners0 = corner_copies(28, DISPLACED)

    below, above, z_below, z_above = working(8, 256)

    def build(group, x, _):
        def tiles(e):
            t, g = E[e, x, 0], swap(E[e, x, 1])
            return jnp.where(upper, t, g), jnp.where(upper, g, t)

        strips = tiles(strip_of(group))
        for n, (e, w, s) in enumerate(fields_of(group)):
            pair = tiles(e)
            for t in range(2):
                halo = pltpu.roll(strips[t], (128 - 16 * n - 8) % 128, 1)
                v = jnp.concatenate([pair[t], halo], axis=1)
                W[w, x, t] = v
                if s == 1:
                    WZ[w, x, t] = z_below(v)
                elif group == SPUN:
                    WZ[w, x, t] = z_above(v)
        return 0

    build0 = functools.partial(build, DISPLACED)
    build1 = functools.partial(build, SPUN)

    def unpack_planes(group):
        for e in arrays_of(group):
            for i in range(2):
                v = RX[i, e]
                E[e, 10 + 2 * i, 0], E[e, 11 + 2 * i, 0] = v, swap(v)
                E[e, 10 + 2 * i, 1], E[e, 11 + 2 * i, 1] = v, v
                v = RC[i, e]
                E[e, 8 + 6 * i, 1], E[e, 9 + 6 * i, 1] = v, swap(v)

    def before(x):
        return lax.rem(x + 15, 16)

    def after(x):
        return lax.rem(x + 1, 16)

    def pair_of(ref, f, x):
        return ref[f, x, 0], ref[f, x, 1]

    def partner(f, planes, o, tile):
        ref = WZ if o[2] else W
        if o[1]:
            return below(pair_of(ref, f, planes[o[0]]), tile)
        return ref[f, planes[o[0]], tile]

    def bonds(x, _):
        planes = (x, before(x))
        for t in range(2):
            own = [W[3 + k, x, t] for k in range(3)]
            here = W[6, x, t]
            for i, o in enumerate(corner_offsets):
                d = [(0.5 - o[k]) + (partner(10 + k, planes, o, t) - own[k]) for k in range(3)]
                w = here * partner(13, planes, o, t)
                r2 = d[0] * d[0] + d[1] * d[1] + d[2] * d[2]
                inverse = lax.rsqrt(r2)
                stretch = r2 * inverse - bond_length
                J[i, x, t] = w * exchange_scale * jnp.exp(-exchange_decay * stretch)
                P3[i, x, t] = w * jnp.exp(-density_decay * stretch)
                RI[i, x, t] = inverse
        return 0

    lax.fori_loop(0, 8, build0, 0, unroll=2)
    lax.fori_loop(1, 8, bonds, 0)
    for c in xs0 + corners0:
        c.wait()
    unpack_planes(DISPLACED)
    lax.fori_loop(8, 16, build0, 0, unroll=2)
    for c in ys1:
        c.wait()
    for e in arrays_of(SPUN):
        unpack_rows(e)
    corners1 = corner_copies(30, SPUN)
    bonds(0, 0)
    lax.fori_loop(8, 12, bonds, 0)
    lax.fori_loop(13, 16, bonds, 0)

    def upper_bonds(x, _):
        planes = (x, after(x))
        for i, o in enumerate(corner_offsets):
            pair = pair_of(J, i, planes[o[0]])
            if o[2]:
                pair = [z_above(v) for v in pair]
            for t in range(2):
                J1[i, x, t] = above(pair, t) if o[1] else pair[t]
        return 0

    lax.fori_loop(0, 16, upper_bonds, 0, unroll=4)

    lax.fori_loop(0, 8, build1, 0, unroll=2)
    def slope(rho):
        return -0.5 * lax.rsqrt(1.0 + rho)

    def slopes(n, _):
        x = lax.rem(n + 15, 16)
        planes = (x, after(x))
        for t in range(2):
            FS[0, x, t] = slope(functools.reduce(jnp.add, [P3[i, x, t] for i in range(8)]))
        rows = []
        for oy in range(2):
            total = []
            for t in range(2):
                flat = P3[2 * oy, planes[0], t] + P3[4 + 2 * oy, planes[1], t]
                high = P3[2 * oy + 1, planes[0], t] + P3[5 + 2 * oy, planes[1], t]
                total.append(flat + z_above(high))
            rows.append(total)
        for t in range(2):
            v = slope(rows[0][t] + above(rows[1], t))
            FS[1, x, t] = v
            FZ[x, t] = z_below(v)
        return 0

    lax.fori_loop(0, 10, slopes, 0, unroll=5)

    for c in xs1 + corners1:
        c.wait()
    unpack_planes(SPUN)
    lax.fori_loop(8, 16, build1, 0, unroll=2)

    def update(u):
        sector = u if u < 8 else 14 - u
        sub, quarter = sector % 2, sector // 2
        tile = quarter // 2
        scale = 0.5 * (step_time if u == 7 else 0.5 * step_time)
        source, target, step = (7, 0, -1) if sub == 0 else (0, 7, 1)
        coupling = J if sub == 0 else J1
        planes = turned_planes()[u]
        shift = below if sub == 0 else above

        @functools.cache
        def around(k, x):
            found = {}
            for oz in range(2):
                pair = pair_of(WZ if oz else W, source + k, x % 16)
                found[0, oz], found[1, oz] = pair[tile], shift(pair, tile)
            return found

        def cross(a, b):
            return [a[1] * b[2] - a[2] * b[1], a[2] * b[0] - a[0] * b[2], a[0] * b[1] - a[1] * b[0]]

        for x in planes:
            c = [coupling[i, x % 16, tile] for i in range(8)]
            h = []
            for k in range(3):
                total = field[k]
                for i, o in enumerate(corner_offsets):
                    total = total + c[i] * around(k, x + step * o[0])[o[1], o[2]]
                h.append(total * scale)
            s = [W[target + k, x % 16, tile] for k in range(3)]
            once = cross(h, s)
            twice = cross(h, once)
            factor = 2.0 / (1.0 + (h[0] * h[0] + h[1] * h[1] + h[2] * h[2]))
            for k in range(3):
                v = s[k] + factor * (once[k] + twice[k])
                W[target + k, x % 16, tile] = v
                WZ[target + k, x % 16, tile] = z_above(v) if sub == 0 else z_below(v)

    for u in range(15):
        update(u)

    def slope_partner(planes, o, tile):
        x = planes[o[0]]
        pair = (FZ[x, 0], FZ[x, 1]) if o[2] else (FS[1, x, 0], FS[1, x, 1])
        return below(pair, tile) if o[1] else pair[tile]

    def forces(x, _):
        planes = (x, before(x))
        sums = [[None] * 2 for _ in range(3)]
        parts = {}
        for t in range(2):
            own = [W[3 + k, x, t] for k in range(3)]
            spins = [W[k, x, t] for k in range(3)]
            mine = FS[0, x, t]
            for i, o in enumerate(corner_offsets):
                d = [(0.5 - o[k]) + (partner(10 + k, planes, o, t) - own[k]) for k in range(3)]
                align = functools.reduce(jnp.add, [spins[k] * partner(7 + k, planes, o, t) for k in range(3)])
                p = P3[i, x, t]
                g = (-pair_decay * pair_scale * (p * p) - density_decay * p * (mine + slope_partner(planes, o, t))
                     + exchange_decay * J[i, x, t] * align) * RI[i, x, t]
                for k in range(3):
                    v = g * d[k]
                    parts[i, t, k] = v
                    sums[k][t] = v if sums[k][t] is None else sums[k][t] + v
        for k in range(3):
            for t in range(2):
                ACC[k, x, t] = sums[k][t]
            for ox in range(2):
                rows = [[parts[4 * ox + 2 * oy, t, k] + z_above(parts[4 * ox + 2 * oy + 1, t, k]) for t in range(2)]
                        for oy in range(2)]
                for t in range(2):
                    v = rows[0][t] + above(rows[1], t)
                    if ox == 0:
                        ACC[3 + k, x, t] = -v
                    else:
                        ACC[3 + k, planes[1], t] = ACC[3 + k, planes[1], t] - v
        return 0

    lax.fori_loop(0, 9, forces, 0)

    def write(x, _):
        for f in range(6):
            for ref, at, out in ((W, 7 * (f // 3) + f % 3, out_s), (ACC, f, out_f)):
                a, b = ref[at, x, 0], ref[at, x, 1]
                out[f // 3, f % 3, x] = jnp.where(upper, a[:, :128], b[:, :128])
        return 0

    lax.fori_loop(0, 8, write, 0, unroll=4)


def emit(spins, forces, out_s, out_f):
    out_s[...] = spins[...]
    out_f[...] = forces[...]


def on_device(sizes, spin_vectors, displacement, occupied, applied_field):
    vmem = pl.BlockSpec(memory_space=pltpu.VMEM)
    hbm = pl.BlockSpec(memory_space=pltpu.HBM)
    smem = pl.BlockSpec(memory_space=pltpu.SMEM)
    shape = jax.ShapeDtypeStruct(spin_vectors.shape, jnp.float32)

    def buffer(*lead):
        return pltpu.VMEM(lead + (8, 128), jnp.float32)

    def wide(*lead):
        return pltpu.VMEM(lead + (16, 2, 8, 256), jnp.float32)

    results = pl.pallas_call(
        functools.partial(kernel, sizes),
        out_shape=(pltpu.VMEM(shape.shape, jnp.float32),) * 2,
        in_specs=[hbm, hbm, hbm, smem],
        out_specs=(vmem, vmem),
        scratch_shapes=[
            buffer(ARRAYS, 16, 2),
            buffer(2, 8), buffer(2, 2, 8),
            buffer(UP[-1]), buffer(UP[-1]),
            buffer(DOWN[-1]), buffer(DOWN[-1]),
            buffer(2, ARRAYS), buffer(2, ARRAYS),
            buffer(2, ARRAYS), buffer(2, ARRAYS),
            wide(14), wide(14), wide(8), wide(8), wide(8), wide(8), wide(2), wide(), wide(6),
            pltpu.VMEM(spin_vectors.shape, jnp.float32),
            pltpu.VMEM(displacement.shape, jnp.float32),
            pltpu.VMEM(occupied.shape, jnp.int32),
            pltpu.SemaphoreType.DMA((32,)),
            pltpu.SemaphoreType.DMA((32,)),
            pltpu.SemaphoreType.DMA((3,)),
        ],
        compiler_params=pltpu.CompilerParams(
            collective_id=0, has_side_effects=True, vmem_limit_bytes=60 * 1024 * 1024),
    )(spin_vectors, displacement, occupied, applied_field)
    return pl.pallas_call(
        emit,
        out_shape=(shape, shape),
        in_specs=[vmem, vmem],
        out_specs=(vmem, vmem),
        compiler_params=pltpu.CompilerParams(vmem_limit_bytes=4 * 1024 * 1024),
    )(*results)


def solution(mesh):
    sizes = tuple(mesh.shape[a] for a in axes)
    block = P(None, None, "gx", "gy", "gz")
    return jax.shard_map(
        functools.partial(on_device, sizes),
        mesh=mesh,
        in_specs=(block, block, P(None, "gx", "gy", "gz"), P()),
        out_specs=(block, block),
        check_vma=False,
    )
```

profile of v0, /device:TPU:1, one launch (start us, length us, event | category | flops | bytes accessed | tf_op | source)
XLA Modules:
  0.0 27.3 jit_solution(2942790766280488298)
XLA Ops:
  0.6 25.9 %shard_map.59 = (f32[2,3,8,8,128]{4,3,2,1,0:T(8,128)S(1)}, f32[2,3,8,8,128]{4,3,2,1,0:T(8,128)S(1)}) custom-call(f32[2,3,8,8,128]{4,3,2,1,0:T(8,128)} %spin_in.1, f32[2,3,8,8,128]{4,3,2,1,0:T(8,128)} %disp_in.1, s32[2,8,8,128]{3,2,1,0:T(8,128)} %occ_in.1, f32[3]{0:T(128)} %field.1), custom_call_target="tpu_custom_call" | custom-call | tf_op jit(solution)/shard_map/pallas_call | solution.py:482
  26.5 0.8 %shard_map.60 = (f32[2,3,8,8,128]{4,3,2,1,0:T(8,128)}, f32[2,3,8,8,128]{4,3,2,1,0:T(8,128)}) custom-call(f32[2,3,8,8,128]{4,3,2,1,0:T(8,128)S(1)} %get-tuple-element.4.spins, f32[2,3,8,8,128]{4,3,2,1,0:T(8,128)S(1)} %get-tuple-element.5.forces), custom_call_target="tpu_custom_call" | custom-call | tf_op jit(solution)/shard_map/pallas_call | solution.py:505
where the time goes:
time: 27.4 us; the launch traced here: 27.3 us
  Pallas kernels  26.6 us (97%)
  between operations  0.64 us (2%)
    pallas_call x1, Pallas kernels, on_device(): pl.pallas_call(functools.partial(kernel, sizes), out_shape=(pltpu.VMEM(sh...  25.9 us
    pallas_call x1, Pallas kernels, on_device(): pl.pallas_call(emit, out_shape=(shape, shape), in_specs=[vmem, vmem], out...  0.77 us

commit v1 on v0

v1 whole, which is shorter than its diff:
```python
import functools
import itertools

import jax
import jax.numpy as jnp
from jax import lax
from jax.experimental import pallas as pl
from jax.experimental.pallas import tpu as pltpu
from jax.sharding import PartitionSpec as P

step_time = 0.6
exchange_scale = 0.35
exchange_decay = 4.0
pair_scale = 0.5
pair_decay = 6.0
density_decay = 3.0
bond_length = 0.8660254037844386
corner_offsets = list(itertools.product((0, 1), repeat=3))
axes = ("gx", "gy", "gz")
MESH = pl.DeviceIdType.MESH

DISPLACED, SPUN = 0, 1
GROUPS = ((0, 4), (9, 3))
ARRAYS = 16
S0, D0, S1, D1, FS = 0, 3, 6, 9, 12
PLACE = {w: w - w // 7 for w in range(14) if w % 7 != 6}
SENSE = (-1,) * 3 + (0,) * 3 + (1,) * 7
FAR = 1000.0


def fields_of(group):
    first, n = GROUPS[group]
    return [(first + n * s + f, 7 * s + f + (3 if group == DISPLACED else 0), s) for s in range(2) for f in range(n)]


def strip_of(group):
    first, n = GROUPS[group]
    return first + 2 * n


TO_BELOW = tuple(
    [(i // 4, i, 0, 2, 2 * (i % 4)) for i in range(8)] + [(2, 2 + i, 2, 2, 2 * i) for i in range(4)])
TO_ABOVE_0 = tuple([(0, i, 7, 1, i) for i in range(8)] + [(1, 2 + i, 5, 2, 2 * i) for i in range(4)])
TO_ABOVE_1 = tuple(
    [(i // 4, i, 6, 2, 2 * (i % 4)) for i in range(8)] + [(2, 2 + i, 4, 2, 2 * i) for i in range(4)])


@functools.cache
def turned_planes():
    need = {(0, x, y) for x in range(9) for y in range(9)} | {(1, x, y) for x in range(-1, 8) for y in range(-1, 8)}
    need |= {(b, x, y) for b in (0, 1) for x in range(8) for y in range(8)}
    planes = {}
    for u in reversed(range(15)):
        sector = u if u < 8 else 14 - u
        sub, quarter = sector % 2, sector // 2
        turned = [k for k in need if k[0] == sub and k[1] // 4 % 2 + 2 * (k[2] // 4 % 2) == quarter]
        planes[u] = sorted({k[1] for k in turned})
        for _, x, y in turned:
            for a, b, _ in corner_offsets:
                need.add((1, x - a, y - b) if sub == 0 else (0, x + a, y + b))
    return planes


def working():
    rows = 8
    row = lax.broadcasted_iota(jnp.int32, (rows, 128), 0)
    first, last = row % 4 == 0, row % 4 == 3

    def turn(v, n):
        return pltpu.roll(v, n % rows, 0)

    def below(pair, tile):
        a, b = pair
        if tile == 0:
            return jnp.where(first, turn(b, 5), turn(a, 1))
        return jnp.where(first, turn(a, 1), turn(b, 1))

    def above(pair, tile):
        a, b = pair
        if tile == 0:
            return jnp.where(last, turn(b, -1), turn(a, -1))
        return jnp.where(last, turn(a, 3), turn(b, -1))

    return below, above


def place_rows():
    up, down, at, n_up, n_down = [], [], [], 0, 0
    for group in (DISPLACED, SPUN):
        for s in [s for _, _, s in fields_of(group)] + [1]:
            up.append(n_up)
            down.append(n_down)
            at.append(s)
            n_up += 2 + s
            n_down += 3
    return up + [n_up], down + [n_down], at


UP, DOWN, GEOMETRY = place_rows()


def kernel(sizes, spin_in, disp_in, occ_in, field_in, out_s, out_f, E, PZ, RZ, SU, RU, SD, RD, SX, RX, SC, RC, U, UZ, XR, XZ, N, NZ, NR, NX, HALO, LR, TMP, J, J1, P3, RI,
           F0, HP, ACC, spin, disp, occ, field, send_sem, recv_sem, load_sem):
    nx, ny, nz = sizes
    me = {a: lax.axis_index(a) for a in axes}
    count = dict(zip(axes, sizes))

    def peer(axis, step):
        n = count[axis]
        return {axis: lax.rem(me[axis] + (n + step), n)}

    peers = []
    for axis in axes:
        peers.append(peer(axis, 1))
        if count[axis] > 2:
            peers.append(peer(axis, -1))
    barrier = pltpu.get_barrier_semaphore()
    for p in peers:
        pl.semaphore_signal(barrier, inc=1, device_id=p, device_id_type=MESH)

    loads = [pltpu.make_async_copy(a, b, load_sem.at[i])
             for i, (a, b) in enumerate(((spin_in, spin), (disp_in, disp), (occ_in, occ)))]
    for c in loads:
        c.start()
    field_load = pltpu.make_async_copy(field_in, field, load_sem.at[3])
    field_load.start()
    for c in loads:
        c.wait()

    lane = lax.broadcasted_iota(jnp.int32, (8, 128), 1)
    row = lax.broadcasted_iota(jnp.int32, (8, 128), 0)
    upper = row < 4

    def swap(v):
        return pltpu.roll(v, 4, 0)

    def load_own(x, _):
        for group in (DISPLACED, SPUN):
            packed = jnp.zeros((8, 128), jnp.float32)
            for n, (e, w, s) in enumerate(fields_of(group)):
                f = w % 7
                if f < 3:
                    v = spin[s, f, x]
                elif f < 6:
                    v = disp[s, f - 3, x]
                else:
                    v = occ[s, x].astype(jnp.float32)
                E[e, x, 0] = v
                packed = jnp.where(lane // 16 == n, pltpu.roll(v, (8 + 16 * n) % 128, 1), packed)
            PZ[group, x] = packed
        return 0

    lax.fori_loop(0, 8, load_own, 0, unroll=2)
    inner = (row >= 2) & (row < 6)

    def routes(e):
        return ((SU, RU, UP[e], (TO_ABOVE_0, TO_ABOVE_1)[GEOMETRY[e]]), (SD, RD, DOWN[e], TO_BELOW))

    def pack_rows(e):
        own = [E[e, x, 0] for x in range(8)]
        for out, _unused, first, pieces in routes(e):
            tiles = {}
            for tile, x, low, n, to in pieces:
                v = pltpu.roll(own[x], (to - low) % 8, 0)
                tiles[tile] = jnp.where(row < to, tiles[tile], v) if to else v
            for tile, v in tiles.items():
                out[first + tile] = v
        SX[0, e] = jnp.where(inner, own[2], swap(own[3]))
        SX[1, e] = jnp.where(inner, own[4], swap(own[5]))

    def unpack_rows(e):
        rows = [jnp.zeros((8, 128), jnp.float32)] * 8
        for _unused, arrived, first, pieces in routes(e):
            for tile, x, low, n, to in pieces:
                v = pltpu.roll(arrived[first + tile], (low - to) % 8, 0)
                rows[x] = jnp.where((row >= low) & (row < low + n), v, rows[x])
        for x in range(8):
            E[e, x, 1] = swap(rows[x])
        SC[0, e] = jnp.where(inner, swap(rows[1]), rows[0])
        SC[1, e] = jnp.where(inner, swap(rows[7]), rows[6])

    def arrays_of(group):
        return range(GROUPS[group][0], strip_of(group) + 1)

    for group in (DISPLACED, SPUN):
        for e, _, _ in fields_of(group):
            pack_rows(e)
    pl.semaphore_wait(barrier, len(peers))

    def send(i, src, dst, to):
        c = pltpu.make_async_remote_copy(
            src_ref=src, dst_ref=dst, send_sem=send_sem.at[i], recv_sem=recv_sem.at[i],
            device_id=to, device_id_type=MESH)
        c.start()
        return c

    def exchange_y(i, lo, hi):
        up = pl.ds(UP[lo], UP[hi] - UP[lo])
        down = pl.ds(DOWN[lo], DOWN[hi] - DOWN[lo])
        return [
            send(i, SD.at[down], RD.at[down], peer("gy", -1)),
            send(i + 1, SU.at[up], RU.at[up], peer("gy", 1)),
        ]

    def exchange_x(i, lo, hi):
        part = pl.ds(lo, hi - lo)

        def plane(x):
            return E.at[part, pl.ds(x, 2), 0]

        return [
            send(i, plane(0), plane(8), peer("gx", -1)),
            send(i + 1, plane(6), plane(14), peer("gx", 1)),
            send(i + 2, SX.at[0, part], RX.at[0, part], peer("gx", -1)),
            send(i + 3, SX.at[1, part], RX.at[1, part], peer("gx", 1)),
        ]

    def exchange_z(i, group):
        found = [send(i, PZ.at[group], RZ.at[0, group], peer("gz", -1))]
        if nz > 2:
            found.append(send(i + 1, PZ.at[group], RZ.at[1, group], peer("gz", 1)))
        return found

    def take_strips(group, copies):
        for c in copies:
            c.wait()
        for x in range(8):
            v = RZ[0, group, x]
            if nz > 2:
                v = jnp.where(lane % 16 < 8, RZ[1, group, x], v)
            E[strip_of(group), x, 0] = v
        pack_rows(strip_of(group))

    def corner_copies(i, group):
        part = pl.ds(GROUPS[group][0], len(arrays_of(group)))
        return [send(i + n, SC.at[n, part], RC.at[n, part], peer("gx", 2 * n - 1)) for n in range(2)]

    z0 = exchange_z(0, DISPLACED)
    ys0 = exchange_y(4, GROUPS[0][0], strip_of(0))
    xs0 = exchange_x(12, GROUPS[0][0], strip_of(0))
    z1 = exchange_z(2, SPUN)
    ys1 = exchange_y(8, GROUPS[1][0], GROUPS[1][0] + 1)
    xs1 = exchange_x(20, GROUPS[1][0], strip_of(1))
    take_strips(DISPLACED, z0)
    ys0 += exchange_y(6, strip_of(0), strip_of(0) + 1)
    ys1 += exchange_y(32, GROUPS[1][0] + 1, strip_of(1))
    xs0 += exchange_x(16, strip_of(0), strip_of(0) + 1)
    take_strips(SPUN, z1)
    ys1 += exchange_y(10, strip_of(1), strip_of(1) + 1)
    xs1 += exchange_x(24, strip_of(1), strip_of(1) + 1)

    below, above = working()
    segment = lane // 32
    third, quarter_low = lane % 16 >= 8, lane // 16

    def lane_roll(v, n):
        return pltpu.roll(v, n % 128, 1)

    def edge_of(halo, p, s):
        return lane_roll(halo, -(32 * p + 7) if s > 0 else 103 - 32 * p)

    def shifted(main, halo, p, s):
        return jnp.where(lane == (0 if s > 0 else 127), edge_of(halo, p, s), lane_roll(main, s))

    def spread(f, q, t, halo, s):
        U[f, 16 + q, t] = halo
        UZ[f, 16 + q, t] = lane_roll(halo, s)
        XR[f, q, t] = lane_roll(halo, 32 * s)
        XZ[f, q, t] = lane_roll(halo, 33 * s)

    def neighbour(now, other, s):
        return jnp.where(segment == (0 if s > 0 else 3), other, now)

    def halves(group, planes, j):
        fields = [(n, e, w) for n, (e, w, s) in enumerate(fields_of(group)) if w % 7 != 6]
        members = list(enumerate(fields_of(group)))
        groups = {}
        for x in planes:
            groups.setdefault(x // 4, []).append(x)
        lone = range(10, 14)

        def put(ref, kept, f, unit, v):
            if j == 0 and unit in lone:
                ref[f, unit, 0], ref[f, unit, 1] = v, v
            elif j == 0:
                kept[f, unit] = v
            else:
                own = kept[f, unit]
                ref[f, unit, 0], ref[f, unit, 1] = jnp.where(upper, own, v), jnp.where(upper, v, own)

        def main_of(x, e, w):
            if w % 7 == 3:
                return jnp.where(E[e + 3, x, j] > 0.5, E[e, x, j], FAR if w < 7 else -FAR)
            return E[e, x, j]

        for x in planes:
            for n, (e, w, _s) in members:
                TMP[n, x] = lane_roll(E[e, x, j], 8 + 16 * n)
                if w % 7 != 6:
                    put(U, N, PLACE[w], x, main_of(x, e, w))
        for x in planes:
            strips = E[strip_of(group), x, j]
            edges = jnp.zeros((8, 128), jnp.float32)
            for n, _m in members:
                edges = jnp.where(quarter_low == n, TMP[n, x], edges)
            for side, v in enumerate((jnp.where(third, edges, strips), jnp.where(third, strips, edges))):
                if group == DISPLACED:
                    held = lane_roll(v, -48) > 0.5
                    v = jnp.where((quarter_low % 4 == 0) & ~held, jnp.where(lane < 64, FAR, -FAR), v)
                LR[side, x] = v
        for x in planes:
            low, high = LR[0, x], LR[1, x]
            for n, _e, _w in fields:
                at = 32 * (x % 4) - 16 * n
                TMP[n, x] = jnp.where(quarter_low % 2 == 0, lane_roll(low, at), lane_roll(high, at + 16))
        for q, places in groups.items():
            for n, e, w in fields:
                f = PLACE[w]
                v = TMP[n, places[0]]
                for x in places[1:]:
                    v = jnp.where(segment == x % 4, TMP[n, x], v)
                HALO[f, q] = v
                put(U, N, f, 16 + q, v)
        for q, places in groups.items():
            for n, e, w in fields:
                f = PLACE[w]
                s = SENSE[f]
                if s:
                    v = HALO[f, q]
                    put(UZ, NZ, f, 16 + q, lane_roll(v, s))
                    put(XR, NR, f, q, lane_roll(v, 32 * s))
                    put(XZ, NX, f, q, lane_roll(v, 33 * s))
                    for x in places:
                        put(UZ, NZ, f, x, shifted(main_of(x, e, w), v, x % 4, s))

    def unpack_planes(group):
        for e in arrays_of(group):
            for i in range(2):
                v = RX[i, e]
                E[e, 10 + 2 * i, 0], E[e, 11 + 2 * i, 0] = v, swap(v)

    def unpack_corners(group):
        for e in arrays_of(group):
            for i in range(2):
                v = RC[i, e]
                E[e, 8 + 6 * i, 1], E[e, 9 + 6 * i, 1] = swap(v), v

    def before(x):
        return lax.rem(x + 15, 16)

    def after(x):
        return lax.rem(x + 1, 16)

    def group_at(q, n):
        return (q + n) % 4 if isinstance(q, int) else lax.rem(q + n, 4)

    def main_pair(f, x, oz):
        ref = UZ if oz else U
        return ref[f, x, 0], ref[f, x, 1]

    def halo_pair(f, q, ox, oz):
        if ox == 0:
            return main_pair(f, 16 + q, oz)
        ref = XZ if oz else XR
        s = SENSE[f]
        other = group_at(q, 3 if s > 0 else 1)
        return tuple(neighbour(ref[f, q, t], ref[f, other, t], s) for t in range(2))

    def bond_of(get, here, t, o):
        d = []
        for k in range(3):
            pair = get(D1 + k, o[0], o[2])
            v = below(pair, t) if o[1] else pair[t]
            d.append((v - here[k]) + (0.5 - o[k]))
        return d

    def bonds(get, unit):
        for t in range(2):
            here = [U[D0 + k, unit, t] for k in range(3)]
            for i, o in enumerate(corner_offsets):
                d = bond_of(get, here, t, o)
                r2 = d[0] * d[0] + d[1] * d[1] + d[2] * d[2]
                inverse = lax.rsqrt(r2)
                stretch = r2 * inverse - bond_length
                J[i, unit, t] = (0.25 * step_time * exchange_scale) * jnp.exp(-exchange_decay * stretch)
                P3[i, unit, t] = jnp.exp(-density_decay * stretch)
                RI[i, unit, t] = inverse

    def main_get(x):
        planes = (x, before(x))
        return lambda f, ox, oz: main_pair(f, planes[ox], oz)

    def halo_get(q):
        return lambda f, ox, oz: halo_pair(f, q, ox, oz)

    def main_bonds(x, _):
        bonds(main_get(x), x)
        return 0

    def halo_bonds(q, _):
        bonds(halo_get(q), 16 + q)
        return 0

    near, far, corner = tuple(range(8)), (8, 9, 10, 11, 13, 14, 15), (8, 9, 14, 15)
    halves(DISPLACED, near, 0)
    halves(SPUN, near, 0)
    for c in xs0:
        c.wait()
    unpack_planes(DISPLACED)
    halves(DISPLACED, far, 0)
    for c in xs1:
        c.wait()
    unpack_planes(SPUN)
    halves(SPUN, far, 0)
    for c in ys0:
        c.wait()
    for e in arrays_of(DISPLACED):
        unpack_rows(e)
    corners0 = corner_copies(28, DISPLACED)
    halves(DISPLACED, near, 1)
    lax.fori_loop(1, 8, main_bonds, 0)
    halo_bonds(1, 0)
    for c in ys1:
        c.wait()
    for e in arrays_of(SPUN):
        unpack_rows(e)
    corners1 = corner_copies(30, SPUN)
    for c in corners0:
        c.wait()
    unpack_corners(DISPLACED)
    halves(DISPLACED, corner, 1)
    main_bonds(0, 0)
    lax.fori_loop(8, 12, main_bonds, 0)
    lax.fori_loop(13, 16, main_bonds, 0)
    lax.fori_loop(2, 5, lambda n, c: halo_bonds(group_at(n, 0), c), 0)

    def halo_above(ref, i, q, ox, oz):
        if ox == 0:
            return [lane_roll(ref[i, 16 + q, t], -oz) if oz else ref[i, 16 + q, t] for t in range(2)]
        return [neighbour(lane_roll(ref[i, 16 + q, t], -32 - oz), lane_roll(ref[i, 16 + group_at(q, 1), t], -32 - oz), -1)
                for t in range(2)]

    def upper_bonds(q, _):
        following = group_at(q, 1)
        for i, o in enumerate(corner_offsets):
            pair = halo_above(J, i, q, o[0], o[2])
            for t in range(2):
                J1[i, 16 + q, t] = above(pair, t) if o[1] else pair[t]
            for p in range(4):
                n = p + o[0]
                x = 4 * q + n if n < 4 else 4 * following
                halo = 16 + (q if n < 4 else following)
                pair = [J[i, x, t] for t in range(2)]
                if o[2]:
                    pair = [shifted(pair[t], J[i, halo, t], n % 4, -1) for t in range(2)]
                for t in range(2):
                    J1[i, 4 * q + p, t] = above(pair, t) if o[1] else pair[t]
        return 0

    for q in range(4):
        upper_bonds(q, 0)

    halves(SPUN, near, 1)

    def slope(rho):
        return -0.5 * lax.rsqrt(1.0 + rho)

    def slopes(q, places):
        following = group_at(q, 1)
        if q < 3:
            for unit in [16 + q] + [4 * q + p for p in places]:
                for t in range(2):
                    F0[unit, t] = slope(functools.reduce(jnp.add, [P3[i, unit, t] for i in range(8)]))
        high = []
        rows = []
        for oy in range(2):
            far = [halo_above(P3, 4 + 2 * oy + oz, q, 1, 0) for oz in range(2)]
            flat = [P3[2 * oy, 16 + q, t] + far[0][t] for t in range(2)]
            high.append([P3[2 * oy + 1, 16 + q, t] + far[1][t] for t in range(2)])
            rows.append([flat[t] + lane_roll(high[oy][t], -1) for t in range(2)])
        halo = [slope(rows[0][t] + above(rows[1], t)) for t in range(2)]
        for t in range(2):
            spread(FS, q, t, halo[t], 1)
        for p in places:
            x = 4 * q + p
            x1 = 4 * q + p + 1 if p < 3 else 4 * following
            rows = []
            for oy in range(2):
                total = []
                for t in range(2):
                    flat = P3[2 * oy, x, t] + P3[4 + 2 * oy, x1, t]
                    top = P3[2 * oy + 1, x, t] + P3[5 + 2 * oy, x1, t]
                    total.append(flat + shifted(top, high[oy][t], p, -1))
                rows.append(total)
            for t in range(2):
                v = slope(rows[0][t] + above(rows[1], t))
                U[FS, x, t] = v
                UZ[FS, x, t] = shifted(v, halo[t], p, 1)

    for q, places in ((3, (3,)), (0, range(4)), (1, range(4)), (2, (0,))):
        slopes(q, places)

    for c in corners1:
        c.wait()
    unpack_corners(SPUN)
    halves(SPUN, corner, 1)
    field_load.wait()
    outer = [(0.25 * step_time) * field[k] for k in range(3)]

    def cross(a, b):
        return [a[1] * b[2] - a[2] * b[1], a[2] * b[0] - a[0] * b[2], a[0] * b[1] - a[1] * b[0]]

    def update(u):
        sector = u if u < 8 else 14 - u
        sub, quarter = sector % 2, sector // 2
        tile = quarter // 2
        source, target, step = (S1, S0, -1) if sub == 0 else (S0, S1, 1)
        coupling = J if sub == 0 else J1
        planes = turned_planes()[u]
        shift = below if sub == 0 else above
        s_new = SENSE[target]

        @functools.cache
        def around(k, x):
            found = {}
            for oz in range(2):
                pair = main_pair(source + k, x % 16, oz)
                found[0, oz], found[1, oz] = pair[tile], shift(pair, tile)
            return found

        def turned(get, unit):
            c = [coupling[i, unit, tile] for i in range(8)]
            h = []
            for k in range(3):
                total = outer[k]
                for i, o in enumerate(corner_offsets):
                    total = total + c[i] * get(k, o)
                h.append(total + total if u == 7 else total)
            s = [U[target + k, unit, tile] for k in range(3)]
            once = cross(h, s)
            twice = cross(h, once)
            factor = 2.0 / (1.0 + (h[0] * h[0] + h[1] * h[1] + h[2] * h[2]))
            return [s[k] + factor * (once[k] + twice[k]) for k in range(3)]

        halos = {}
        for q in sorted({x % 16 // 4 for x in planes}):
            found = {}
            for k in range(3):
                for ox in range(2):
                    for oz in range(2):
                        pair = halo_pair(source + k, q, ox, oz)
                        found[k, ox, 0, oz], found[k, ox, 1, oz] = pair[tile], shift(pair, tile)
            halos[q] = turned(lambda k, o: found[k, o[0], o[1], o[2]], 16 + q)
            for k in range(3):
                spread(target + k, q, tile, halos[q][k], s_new)
        for x in planes:
            unit = x % 16
            v = turned(lambda k, o: around(k, x + step * o[0])[o[1], o[2]], unit)
            for k in range(3):
                U[target + k, unit, tile] = v[k]
                UZ[target + k, unit, tile] = shifted(v[k], halos[unit // 4][k], unit % 4, s_new)

    for u in range(15):
        update(u)

    def strength(get, unit, t, i, o, here, spins, mine):
        d = bond_of(get, here, t, o)

        def at(f):
            pair = get(f, o[0], o[2])
            return below(pair, t) if o[1] else pair[t]

        align = functools.reduce(jnp.add, [spins[k] * at(S1 + k) for k in range(3)])
        p = P3[i, unit, t]
        g = (-density_decay * p * (p * (pair_decay * pair_scale / density_decay) + (mine + at(FS)))
             + (exchange_decay / (0.25 * step_time)) * J[i, unit, t] * align) * RI[i, unit, t]
        return [g * d[k] for k in range(3)]

    def of_unit(unit, t):
        return [U[D0 + k, unit, t] for k in range(3)], [U[S0 + k, unit, t] for k in range(3)], F0[unit, t]

    def halo_forces(q, _):
        for t in range(2):
            own = of_unit(16 + q, t)
            for i, o in enumerate(corner_offsets):
                if o[2]:
                    v = strength(halo_get(q), 16 + q, t, i, o, *own)
                    for k in range(3):
                        HP[i // 2, k, q, t] = v[k]
        return 0

    lax.fori_loop(0, 3, halo_forces, 0)

    def forces(x, q, p):
        planes = (x, before(x))
        sums = [[None] * 2 for _ in range(3)]
        parts = {}
        for t in range(2):
            own = of_unit(x, t)
            for i, o in enumerate(corner_offsets):
                v = strength(main_get(x), x, t, i, o, *own)
                for k in range(3):
                    parts[i, t, k] = v[k]
                    sums[k][t] = v[k] if sums[k][t] is None else sums[k][t] + v[k]
        for k in range(3):
            for t in range(2):
                ACC[k, x, t] = sums[k][t]
            for ox in range(2):
                rows = [[parts[4 * ox + 2 * oy, t, k] + shifted(parts[4 * ox + 2 * oy + 1, t, k], HP[2 * ox + oy, k, q, t], p, -1) for t in range(2)]
                        for oy in range(2)]
                for t in range(2):
                    v = rows[0][t] + above(rows[1], t)
                    if ox == 0:
                        ACC[3 + k, x, t] = -v
                    else:
                        ACC[3 + k, planes[1], t] = ACC[3 + k, planes[1], t] - v

    def four_forces(q, _):
        for p in range(4):
            forces(4 * q + p, q, p)
        return 0

    lax.fori_loop(0, 2, four_forces, 0)
    forces(8, 2, 0)

    def write(x, _):
        for f in range(6):
            for ref, at, out in ((U, (S1 if f > 2 else S0) + f % 3, out_s), (ACC, f, out_f)):
                out[f // 3, f % 3, x] = jnp.where(upper, ref[at, x, 0], ref[at, x, 1])
        return 0

    lax.fori_loop(0, 8, write, 0, unroll=4)


def emit(spins, forces, out_s, out_f, sem):
    copies = [pltpu.make_async_copy(a, b, sem.at[i]) for i, (a, b) in enumerate(((spins, out_s), (forces, out_f)))]
    for c in copies:
        c.start()
    for c in copies:
        c.wait()


def on_device(sizes, spin_vectors, displacement, occupied, applied_field):
    vmem = pl.BlockSpec(memory_space=pltpu.VMEM)
    hbm = pl.BlockSpec(memory_space=pltpu.HBM)
    shape = jax.ShapeDtypeStruct(spin_vectors.shape, jnp.float32)

    def buffer(*lead):
        return pltpu.VMEM(lead + (8, 128), jnp.float32)

    results = pl.pallas_call(
        functools.partial(kernel, sizes),
        out_shape=(pltpu.VMEM(shape.shape, jnp.float32),) * 2,
        in_specs=[hbm, hbm, hbm, hbm],
        out_specs=(vmem, vmem),
        scratch_shapes=[
            buffer(ARRAYS, 16, 2),
            buffer(2, 8), buffer(2, 2, 8),
            buffer(UP[-1]), buffer(UP[-1]),
            buffer(DOWN[-1]), buffer(DOWN[-1]),
            buffer(2, ARRAYS), buffer(2, ARRAYS),
            buffer(2, ARRAYS), buffer(2, ARRAYS),
            buffer(13, 20, 2), buffer(13, 20, 2), buffer(13, 4, 2), buffer(13, 4, 2), buffer(12, 20), buffer(12, 20), buffer(12, 4), buffer(12, 4), buffer(12, 4), buffer(2, 16), buffer(8, 16),
            buffer(8, 20, 2), buffer(8, 20, 2), buffer(8, 20, 2), buffer(8, 20, 2),
            buffer(20, 2), buffer(4, 3, 4, 2), buffer(6, 16, 2),
            pltpu.VMEM(spin_vectors.shape, jnp.float32),
            pltpu.VMEM(displacement.shape, jnp.float32),
            pltpu.VMEM(occupied.shape, jnp.int32),
            pltpu.SMEM(applied_field.shape, jnp.float32),
            pltpu.SemaphoreType.DMA((34,)),
            pltpu.SemaphoreType.DMA((34,)),
            pltpu.SemaphoreType.DMA((4,)),
        ],
        compiler_params=pltpu.CompilerParams(
            collective_id=0, has_side_effects=True, vmem_limit_bytes=60 * 1024 * 1024),
    )(spin_vectors, displacement, occupied, applied_field)
    return pl.pallas_call(
        emit,
        out_shape=(shape, shape),
        in_specs=[vmem, vmem],
        out_specs=(hbm, hbm),
        scratch_shapes=[pltpu.SemaphoreType.DMA((2,))],
        compiler_params=pltpu.CompilerParams(vmem_limit_bytes=4 * 1024 * 1024),
    )(*results)


def solution(mesh):
    sizes = tuple(mesh.shape[a] for a in axes)
    block = P(None, None, "gx", "gy", "gz")
    return jax.shard_map(
        functools.partial(on_device, sizes),
        mesh=mesh,
        in_specs=(block, block, P(None, "gx", "gy", "gz"), P()),
        out_specs=(block, block),
        check_vma=False,
    )
```

time: 27.4 us -> 24.6 us (0.90)
  Pallas kernels: 26.6 us -> 23.8 us
    pallas_call x1, Pallas kernels: 25.9 us -> 23 us  [on_device(): pl.pallas_call(functools.partial(kernel, sizes), out_shape=(pltpu.VMEM(sh...]
where the time goes in v1:
time: 24.6 us; the launch traced here: 24.4 us
  Pallas kernels  23.8 us (97%)
  between operations  0.64 us (3%)
    pallas_call x1, Pallas kernels, on_device(): pl.pallas_call(functools.partial(kernel, sizes), out_shape=(pltpu.VMEM(sh...  23 us
    pallas_call x1, Pallas kernels, on_device(): pl.pallas_call(emit, out_shape=(shape, shape), in_specs=[vmem, vmem], out...  0.76 us

profile of v1, /device:TPU:1, one launch (start us, length us, event | category | flops | bytes accessed | tf_op | source)
XLA Modules:
  0.0 24.4 jit_solution(13152791371026172735)
XLA Ops:
  0.6 23.0 %shard_map.59 = (f32[2,3,8,8,128]{4,3,2,1,0:T(8,128)S(1)}, f32[2,3,8,8,128]{4,3,2,1,0:T(8,128)S(1)}) custom-call(f32[2,3,8,8,128]{4,3,2,1,0:T(8,128)} %spin_in.1, f32[2,3,8,8,128]{4,3,2,1,0:T(8,128)} %disp_in.1, s32[2,8,8,128]{3,2,1,0:T(8,128)} %occ_in.1, f32[3]{0:T(128)} %field_in.1), custom_call_target="tpu_custom_call" | custom-call | tf_op jit(solution)/shard_map/pallas_call | solution.py:651
  23.7 0.8 %shard_map.60 = (f32[2,3,8,8,128]{4,3,2,1,0:T(8,128)}, f32[2,3,8,8,128]{4,3,2,1,0:T(8,128)}) custom-call(f32[2,3,8,8,128]{4,3,2,1,0:T(8,128)S(1)} %get-tuple-element.4.spins, f32[2,3,8,8,128]{4,3,2,1,0:T(8,128)S(1)} %get-tuple-element.5.forces), custom_call_target="tpu_custom_call" | custom-call | tf_op jit(solution)/shard_map/pallas_call | solution.py:677

commit v2 on v1

--- a/solution.py
+++ b/solution.py
@@ -119,13 +119,11 @@
         pl.semaphore_signal(barrier, inc=1, device_id=p, device_id_type=MESH)
 
     loads = [pltpu.make_async_copy(a, b, load_sem.at[i])
-             for i, (a, b) in enumerate(((spin_in, spin), (disp_in, disp), (occ_in, occ)))]
+             for i, (a, b) in enumerate(((disp_in, disp), (occ_in, occ), (spin_in, spin)))]
     for c in loads:
         c.start()
     field_load = pltpu.make_async_copy(field_in, field, load_sem.at[3])
     field_load.start()
-    for c in loads:
-        c.wait()
 
     lane = lax.broadcasted_iota(jnp.int32, (8, 128), 1)
     row = lax.broadcasted_iota(jnp.int32, (8, 128), 0)
@@ -134,23 +132,24 @@
     def swap(v):
         return pltpu.roll(v, 4, 0)
 
-    def load_own(x, _):
-        for group in (DISPLACED, SPUN):
+    def load_own(group):
+        for e, w, s in fields_of(group):
+            f = w % 7
+            for x in range(8):
+                if f < 3:
+                    E[e, x, 0] = spin[s, f, x]
+                elif f < 6:
+                    E[e, x, 0] = disp[s, f - 3, x]
+                else:
+                    E[e, x, 0] = occ[s, x].astype(jnp.float32)
+
+    def pack_edges(group):
+        for x in range(8):
             packed = jnp.zeros((8, 128), jnp.float32)
             for n, (e, w, s) in enumerate(fields_of(group)):
-                f = w % 7
-                if f < 3:
-                    v = spin[s, f, x]
-                elif f < 6:
-                    v = disp[s, f - 3, x]
-                else:
-                    v = occ[s, x].astype(jnp.float32)
-                E[e, x, 0] = v
-                packed = jnp.where(lane // 16 == n, pltpu.roll(v, (8 + 16 * n) % 128, 1), packed)
+                packed = jnp.where(lane // 16 == n, pltpu.roll(E[e, x, 0], (8 + 16 * n) % 128, 1), packed)
             PZ[group, x] = packed
-        return 0
-
-    lax.fori_loop(0, 8, load_own, 0, unroll=2)
+
     inner = (row >= 2) & (row < 6)
 
     def routes(e):
@@ -182,11 +181,6 @@
     def arrays_of(group):
         return range(GROUPS[group][0], strip_of(group) + 1)
 
-    for group in (DISPLACED, SPUN):
-        for e, _, _ in fields_of(group):
-            pack_rows(e)
-    pl.semaphore_wait(barrier, len(peers))
-
     def send(i, src, dst, to):
         c = pltpu.make_async_remote_copy(
             src_ref=src, dst_ref=dst, send_sem=send_sem.at[i], recv_sem=recv_sem.at[i],
@@ -235,16 +229,28 @@
         part = pl.ds(GROUPS[group][0], len(arrays_of(group)))
         return [send(i + n, SC.at[n, part], RC.at[n, part], peer("gx", 2 * n - 1)) for n in range(2)]
 
+    loads[0].wait()
+    loads[1].wait()
+    load_own(DISPLACED)
+    for e, _, _ in fields_of(DISPLACED):
+        pack_rows(e)
+    pack_edges(DISPLACED)
+    loads[2].wait()
+    load_own(SPUN)
+    for e, _, _ in fields_of(SPUN):
+        pack_rows(e)
+    pack_edges(SPUN)
+    pl.semaphore_wait(barrier, len(peers))
     z0 = exchange_z(0, DISPLACED)
     ys0 = exchange_y(4, GROUPS[0][0], strip_of(0))
-    xs0 = exchange_x(12, GROUPS[0][0], strip_of(0))
     z1 = exchange_z(2, SPUN)
     ys1 = exchange_y(8, GROUPS[1][0], GROUPS[1][0] + 1)
-    xs1 = exchange_x(20, GROUPS[1][0], strip_of(1))
+    xs0 = exchange_x(12, GROUPS[0][0], strip_of(0))
     take_strips(DISPLACED, z0)
     ys0 += exchange_y(6, strip_of(0), strip_of(0) + 1)
     ys1 += exchange_y(32, GROUPS[1][0] + 1, strip_of(1))
     xs0 += exchange_x(16, strip_of(0), strip_of(0) + 1)
+    xs1 = exchange_x(20, GROUPS[1][0], strip_of(1))
     take_strips(SPUN, z1)
     ys1 += exchange_y(10, strip_of(1), strip_of(1) + 1)
     xs1 += exchange_x(24, strip_of(1), strip_of(1) + 1)
@@ -284,6 +290,8 @@
                 ref[f, unit, 0], ref[f, unit, 1] = v, v
             elif j == 0:
                 kept[f, unit] = v
+                if unit in (8, 9, 14, 15):
+                    ref[f, unit, 0], ref[f, unit, 1] = v, v
             else:
                 own = kept[f, unit]
                 ref[f, unit, 0], ref[f, unit, 1] = jnp.where(upper, own, v), jnp.where(upper, v, own)
@@ -374,10 +382,12 @@
             d.append((v - here[k]) + (0.5 - o[k]))
         return d
 
-    def bonds(get, unit):
+    def bonds(get, unit, crossing=False):
         for t in range(2):
             here = [U[D0 + k, unit, t] for k in range(3)]
             for i, o in enumerate(corner_offsets):
+                if crossing and not o[0]:
+                    continue
                 d = bond_of(get, here, t, o)
                 r2 = d[0] * d[0] + d[1] * d[1] + d[2] * d[2]
                 inverse = lax.rsqrt(r2)
@@ -401,39 +411,6 @@
         bonds(halo_get(q), 16 + q)
         return 0
 
-    near, far, corner = tuple(range(8)), (8, 9, 10, 11, 13, 14, 15), (8, 9, 14, 15)
-    halves(DISPLACED, near, 0)
-    halves(SPUN, near, 0)
-    for c in xs0:
-        c.wait()
-    unpack_planes(DISPLACED)
-    halves(DISPLACED, far, 0)
-    for c in xs1:
-        c.wait()
-    unpack_planes(SPUN)
-    halves(SPUN, far, 0)
-    for c in ys0:
-        c.wait()
-    for e in arrays_of(DISPLACED):
-        unpack_rows(e)
-    corners0 = corner_copies(28, DISPLACED)
-    halves(DISPLACED, near, 1)
-    lax.fori_loop(1, 8, main_bonds, 0)
-    halo_bonds(1, 0)
-    for c in ys1:
-        c.wait()
-    for e in arrays_of(SPUN):
-        unpack_rows(e)
-    corners1 = corner_copies(30, SPUN)
-    for c in corners0:
-        c.wait()
-    unpack_corners(DISPLACED)
-    halves(DISPLACED, corner, 1)
-    main_bonds(0, 0)
-    lax.fori_loop(8, 12, main_bonds, 0)
-    lax.fori_loop(13, 16, main_bonds, 0)
-    lax.fori_loop(2, 5, lambda n, c: halo_bonds(group_at(n, 0), c), 0)
-
     def halo_above(ref, i, q, ox, oz):
         if ox == 0:
             return [lane_roll(ref[i, 16 + q, t], -oz) if oz else ref[i, 16 + q, t] for t in range(2)]
@@ -446,7 +423,7 @@
             pair = halo_above(J, i, q, o[0], o[2])
             for t in range(2):
                 J1[i, 16 + q, t] = above(pair, t) if o[1] else pair[t]
-            for p in range(4):
+            for p in [p for p in range(4) if 4 * q + p not in (11, 12)]:
                 n = p + o[0]
                 x = 4 * q + n if n < 4 else 4 * following
                 halo = 16 + (q if n < 4 else following)
@@ -457,20 +434,16 @@
                     J1[i, 4 * q + p, t] = above(pair, t) if o[1] else pair[t]
         return 0
 
-    for q in range(4):
-        upper_bonds(q, 0)
-
-    halves(SPUN, near, 1)
-
     def slope(rho):
         return -0.5 * lax.rsqrt(1.0 + rho)
 
+    def own_slopes(units):
+        for unit in units:
+            for t in range(2):
+                F0[unit, t] = slope(functools.reduce(jnp.add, [P3[i, unit, t] for i in range(8)]))
+
     def slopes(q, places):
         following = group_at(q, 1)
-        if q < 3:
-            for unit in [16 + q] + [4 * q + p for p in places]:
-                for t in range(2):
-                    F0[unit, t] = slope(functools.reduce(jnp.add, [P3[i, unit, t] for i in range(8)]))
         high = []
         rows = []
         for oy in range(2):
@@ -497,9 +470,49 @@
                 U[FS, x, t] = v
                 UZ[FS, x, t] = shifted(v, halo[t], p, 1)
 
-    for q, places in ((3, (3,)), (0, range(4)), (1, range(4)), (2, (0,))):
+    near, far, corner = tuple(range(8)), tuple(range(8, 16)), (8, 9, 14, 15)
+    halves(DISPLACED, near, 0)
+    halves(SPUN, near, 0)
+    for c in xs0:
+        c.wait()
+    unpack_planes(DISPLACED)
+    halves(DISPLACED, far, 0)
+    for c in ys0:
+        c.wait()
+    for e in arrays_of(DISPLACED):
+        unpack_rows(e)
+    corners0 = corner_copies(28, DISPLACED)
+    halves(DISPLACED, near, 1)
+    lax.fori_loop(0, 8, main_bonds, 0)
+    lax.fori_loop(0, 2, halo_bonds, 0)
+    lax.fori_loop(10, 12, main_bonds, 0)
+    main_bonds(13, 0)
+    upper_bonds(0, 0)
+    slopes(0, range(4))
+    own_slopes((1, 2, 3, 4, 5, 6, 7, 17))
+    for c in xs1:
+        c.wait()
+    unpack_planes(SPUN)
+    halves(SPUN, far, 0)
+    for c in ys1:
+        c.wait()
+    for e in arrays_of(SPUN):
+        unpack_rows(e)
+    corners1 = corner_copies(30, SPUN)
+    halves(SPUN, near, 1)
+    for c in corners0:
+        c.wait()
+    unpack_corners(DISPLACED)
+    halves(DISPLACED, corner, 1)
+    bonds(main_get(0), 0, True)
+    lax.fori_loop(8, 10, main_bonds, 0)
+    lax.fori_loop(14, 16, main_bonds, 0)
+    lax.fori_loop(2, 5, lambda n, c: halo_bonds(group_at(n, 0), c), 0)
+    for q in range(1, 4):
+        upper_bonds(q, 0)
+    for q, places in ((3, (3,)), (1, range(4)), (2, (0,))):
         slopes(q, places)
-
+    own_slopes((0, 8, 16, 18))
     for c in corners1:
         c.wait()
     unpack_corners(SPUN)

time: 24.6 us -> 23.5 us (0.955)
  Pallas kernels: 23.8 us -> 22.8 us
    pallas_call x1, Pallas kernels: 23 us -> 22 us  [on_device(): pl.pallas_call(functools.partial(kernel, sizes), out_shape=(pltpu.VMEM(sh...]
where the time goes in v2:
time: 23.5 us; the launch traced here: 23.4 us
  Pallas kernels  22.8 us (97%)
  between operations  0.64 us (3%)
    pallas_call x1, Pallas kernels, on_device(): pl.pallas_call(functools.partial(kernel, sizes), out_shape=(pltpu.VMEM(sh...  22 us
    pallas_call x1, Pallas kernels, on_device(): pl.pallas_call(emit, out_shape=(shape, shape), in_specs=[vmem, vmem], out...  0.76 us

profile of v2, /device:TPU:1, one launch (start us, length us, event | category | flops | bytes accessed | tf_op | source)
XLA Modules:
  0.0 23.4 jit_solution(12227476761931292018)
XLA Ops:
  0.6 22.0 %shard_map.59 = (f32[2,3,8,8,128]{4,3,2,1,0:T(8,128)S(1)}, f32[2,3,8,8,128]{4,3,2,1,0:T(8,128)S(1)}) custom-call(f32[2,3,8,8,128]{4,3,2,1,0:T(8,128)} %spin_in.1, f32[2,3,8,8,128]{4,3,2,1,0:T(8,128)} %disp_in.1, s32[2,8,8,128]{3,2,1,0:T(8,128)} %occ_in.1, f32[3]{0:T(128)} %field_in.1), custom_call_target="tpu_custom_call" | custom-call | tf_op jit(solution)/shard_map/pallas_call | solution.py:664
  22.6 0.8 %shard_map.60 = (f32[2,3,8,8,128]{4,3,2,1,0:T(8,128)}, f32[2,3,8,8,128]{4,3,2,1,0:T(8,128)}) custom-call(f32[2,3,8,8,128]{4,3,2,1,0:T(8,128)S(1)} %get-tuple-element.4.spins, f32[2,3,8,8,128]{4,3,2,1,0:T(8,128)S(1)} %get-tuple-element.5.forces), custom_call_target="tpu_custom_call" | custom-call | tf_op jit(solution)/shard_map/pallas_call | solution.py:690

commit v3 on v2

--- a/solution.py
+++ b/solution.py
@@ -234,23 +234,23 @@
     load_own(DISPLACED)
     for e, _, _ in fields_of(DISPLACED):
         pack_rows(e)
+    pl.semaphore_wait(barrier, len(peers))
+    ys0 = exchange_y(4, GROUPS[0][0], strip_of(0))
     pack_edges(DISPLACED)
+    z0 = exchange_z(0, DISPLACED)
     loads[2].wait()
     load_own(SPUN)
     for e, _, _ in fields_of(SPUN):
         pack_rows(e)
+    ys1 = exchange_y(8, GROUPS[1][0], GROUPS[1][0] + 1)
     pack_edges(SPUN)
-    pl.semaphore_wait(barrier, len(peers))
-    z0 = exchange_z(0, DISPLACED)
-    ys0 = exchange_y(4, GROUPS[0][0], strip_of(0))
     z1 = exchange_z(2, SPUN)
-    ys1 = exchange_y(8, GROUPS[1][0], GROUPS[1][0] + 1)
     xs0 = exchange_x(12, GROUPS[0][0], strip_of(0))
+    xs1 = exchange_x(20, GROUPS[1][0], strip_of(1))
     take_strips(DISPLACED, z0)
     ys0 += exchange_y(6, strip_of(0), strip_of(0) + 1)
     ys1 += exchange_y(32, GROUPS[1][0] + 1, strip_of(1))
     xs0 += exchange_x(16, strip_of(0), strip_of(0) + 1)
-    xs1 = exchange_x(20, GROUPS[1][0], strip_of(1))
     take_strips(SPUN, z1)
     ys1 += exchange_y(10, strip_of(1), strip_of(1) + 1)
     xs1 += exchange_x(24, strip_of(1), strip_of(1) + 1)
@@ -306,6 +306,10 @@
                 TMP[n, x] = lane_roll(E[e, x, j], 8 + 16 * n)
                 if w % 7 != 6:
                     put(U, N, PLACE[w], x, main_of(x, e, w))
+                if group == SPUN:
+                    s = SENSE[PLACE[w]]
+                    edge = lane_roll(E[strip_of(group), x, j], -16 * n - 7 if s > 0 else 119 - 16 * n)
+                    put(UZ, NZ, PLACE[w], x, jnp.where(lane == (0 if s > 0 else 127), edge, lane_roll(E[e, x, j], s)))
         for x in planes:
             strips = E[strip_of(group), x, j]
             edges = jnp.zeros((8, 128), jnp.float32)
@@ -338,8 +342,9 @@
                     put(UZ, NZ, f, 16 + q, lane_roll(v, s))
                     put(XR, NR, f, q, lane_roll(v, 32 * s))
                     put(XZ, NX, f, q, lane_roll(v, 33 * s))
-                    for x in places:
-                        put(UZ, NZ, f, x, shifted(main_of(x, e, w), v, x % 4, s))
+                    if group == DISPLACED:
+                        for x in places:
+                            put(UZ, NZ, f, x, shifted(main_of(x, e, w), v, x % 4, s))
 
     def unpack_planes(group):
         for e in arrays_of(group):
@@ -477,6 +482,10 @@
         c.wait()
     unpack_planes(DISPLACED)
     halves(DISPLACED, far, 0)
+    for c in xs1:
+        c.wait()
+    unpack_planes(SPUN)
+    halves(SPUN, far, 0)
     for c in ys0:
         c.wait()
     for e in arrays_of(DISPLACED):
@@ -490,10 +499,6 @@
     upper_bonds(0, 0)
     slopes(0, range(4))
     own_slopes((1, 2, 3, 4, 5, 6, 7, 17))
-    for c in xs1:
-        c.wait()
-    unpack_planes(SPUN)
-    halves(SPUN, far, 0)
     for c in ys1:
         c.wait()
     for e in arrays_of(SPUN):
@@ -602,15 +607,18 @@
                         HP[i // 2, k, q, t] = v[k]
         return 0
 
-    lax.fori_loop(0, 3, halo_forces, 0)
-
-    def forces(x, q, p):
+    for q in range(3):
+        halo_forces(q, 0)
+
+    def forces(x, q, p, sides=(0, 1)):
         planes = (x, before(x))
         sums = [[None] * 2 for _ in range(3)]
         parts = {}
         for t in range(2):
             own = of_unit(x, t)
             for i, o in enumerate(corner_offsets):
+                if o[0] not in sides:
+                    continue
                 v = strength(main_get(x), x, t, i, o, *own)
                 for k in range(3):
                     parts[i, t, k] = v[k]
@@ -618,7 +626,7 @@
         for k in range(3):
             for t in range(2):
                 ACC[k, x, t] = sums[k][t]
-            for ox in range(2):
+            for ox in sides:
                 rows = [[parts[4 * ox + 2 * oy, t, k] + shifted(parts[4 * ox + 2 * oy + 1, t, k], HP[2 * ox + oy, k, q, t], p, -1) for t in range(2)]
                         for oy in range(2)]
                 for t in range(2):
@@ -634,7 +642,7 @@
         return 0
 
     lax.fori_loop(0, 2, four_forces, 0)
-    forces(8, 2, 0)
+    forces(8, 2, 0, (1,))
 
     def write(x, _):
         for f in range(6):

time: 23.5 us -> 23.4 us (level)
  no operation moved by 1% of the time
where the time goes in v3:
time: 23.4 us; the launch traced here: 23.3 us
  Pallas kernels  22.6 us (97%)
  between operations  0.64 us (3%)
    pallas_call x1, Pallas kernels, on_device(): pl.pallas_call(functools.partial(kernel, sizes), out_shape=(pltpu.VMEM(sh...  21.9 us
    pallas_call x1, Pallas kernels, on_device(): pl.pallas_call(emit, out_shape=(shape, shape), in_specs=[vmem, vmem], out...  0.76 us

profile of v3, /device:TPU:1, one launch (start us, length us, event | category | flops | bytes accessed | tf_op | source)
XLA Modules:
  0.0 23.3 jit_solution(15224946949834764437)
XLA Ops:
  0.6 21.9 %shard_map.59 = (f32[2,3,8,8,128]{4,3,2,1,0:T(8,128)S(1)}, f32[2,3,8,8,128]{4,3,2,1,0:T(8,128)S(1)}) custom-call(f32[2,3,8,8,128]{4,3,2,1,0:T(8,128)} %spin_in.1, f32[2,3,8,8,128]{4,3,2,1,0:T(8,128)} %disp_in.1, s32[2,8,8,128]{3,2,1,0:T(8,128)} %occ_in.1, f32[3]{0:T(128)} %field_in.1), custom_call_target="tpu_custom_call" | custom-call | tf_op jit(solution)/shard_map/pallas_call | solution.py:672
  22.5 0.8 %shard_map.60 = (f32[2,3,8,8,128]{4,3,2,1,0:T(8,128)}, f32[2,3,8,8,128]{4,3,2,1,0:T(8,128)}) custom-call(f32[2,3,8,8,128]{4,3,2,1,0:T(8,128)S(1)} %get-tuple-element.4.spins, f32[2,3,8,8,128]{4,3,2,1,0:T(8,128)S(1)} %get-tuple-element.5.forces), custom_call_target="tpu_custom_call" | custom-call | tf_op jit(solution)/shard_map/pallas_call | solution.py:698
